TPU v7x, 32 devices: a whole 2x2x4 slice. The times are simulated.
32 devices in a mesh: stage: 2 (over x), data: 16 (over z, y, core).
Axes of the slice: x: 2, y: 2, z: 4, core: 2. Of those that a mesh axis runs over, the one named last changes fastest.
Arguments:
- w_master: float32 [32, 512, 2048], P('stage', 'data'), parts along dimension 0
- momentum: float32 [32, 512, 2048], P('stage', 'data'), parts along dimension 0
- grads: bfloat16 [32, 16, 512, 2048], P(('stage', 'data')), parts along dimension 0
Outputs:
- output 1: float32 [32, 512, 2048], P('stage', 'data'), parts along dimension 0
- output 2: float32 [32, 512, 2048], P('stage', 'data'), parts along dimension 0
There are 2 independent parts. A program takes and returns all parts, laid end to end along the dimension named above; each array names one.
All inputs are finite; a program needn't handle non-finite values.
Results may differ from a plain program's by a relative error of at most 0.0109877.
Values are sent between devices in bfloat16 or wider.
A program may use at most 1 GiB of HBM per device.

v0:
```python
import math
import jax
import jax.numpy as jnp
from jax import lax
from jax.sharding import PartitionSpec as P, NamedSharding

MOMENTUM_COEF = 0.95
LEARN_RATE = 0.05
WEIGHT_DECAY = 0.2
NORM_EPS = 1e-7
COEF_A = 3.4445
COEF_B = -4.7750
COEF_C = 2.0315
NS_ITERS = 5


def newton_schulz(x_cur):
    n_rows, n_cols = x_cur.shape[1], x_cur.shape[2]
    for _ in range(NS_ITERS):
        if n_rows > n_cols:
            gram_f = jnp.einsum('bri,brj->bij', x_cur, x_cur, preferred_element_type=jnp.float32)
        else:
            gram_f = jnp.einsum('bik,bjk->bij', x_cur, x_cur, preferred_element_type=jnp.float32)
        gram_mat = gram_f.astype(jnp.bfloat16)
        gram_sq = jnp.einsum('bij,bjk->bik', gram_mat, gram_mat, preferred_element_type=jnp.float32)
        poly_mat = (COEF_B * gram_mat.astype(jnp.float32) + COEF_C * gram_sq).astype(jnp.bfloat16)
        if n_rows > n_cols:
            poly_x = jnp.einsum('brj,bij->bri', x_cur, poly_mat, preferred_element_type=jnp.float32)
        else:
            poly_x = jnp.einsum('bij,bjk->bik', poly_mat, x_cur, preferred_element_type=jnp.float32)
        x_cur = (COEF_A * x_cur.astype(jnp.float32) + poly_x).astype(jnp.bfloat16)
    return x_cur


def solution(mesh):
    group_size = mesh.shape['data']
    row_spec = P('stage', 'data', None)
    grad_spec = P(('stage', 'data'), None, None, None)

    def local_step(w_rows, mom_rows, grad_full):
        n_mats, rows_dev, n_cols = w_rows.shape
        n_rows = rows_dev * group_size
        per_dev = n_mats // group_size
        my_index = lax.axis_index('data')
        grad_rows = lax.psum_scatter(grad_full[0].astype(jnp.float32), 'data', scatter_dimension=1, tiled=True)
        mom_new = MOMENTUM_COEF * mom_rows + grad_rows
        frob_norm = jnp.sqrt(lax.psum(jnp.sum(mom_new * mom_new, axis=(1, 2)), 'data'))
        owned_mom = lax.all_to_all(mom_new.astype(jnp.bfloat16), 'data', 0, 1, tiled=True)
        owned_norm = lax.dynamic_slice_in_dim(frob_norm, my_index * per_dev, per_dev)
        x_start = (owned_mom.astype(jnp.float32) / (owned_norm[:, None, None] + NORM_EPS)).astype(jnp.bfloat16)
        x_ortho = newton_schulz(x_start)
        x_rows = lax.all_to_all(x_ortho, 'data', 1, 0, tiled=True)
        rms_scale = 0.2 * math.sqrt(max(n_rows, n_cols))
        w_new = w_rows - LEARN_RATE * (x_rows.astype(jnp.float32) * rms_scale + WEIGHT_DECAY * w_rows)
        return w_new, mom_new

    return jax.shard_map(local_step, mesh=mesh, in_specs=(row_spec, row_spec, grad_spec), out_specs=(row_spec, row_spec), check_vma=False)
```

profile of v0, /device:TPU:9, one launch (start us, length us, event | category | flops | bytes accessed | tf_op | source)
XLA Modules:
  0.0 879.4 jit_solution(6453439951054354588)
XLA Ops:
  7.2 0.0 reduce-scatter.2.cloned.1.call-start
  7.2 32.4 %bitcast_convert_fusion = f32[16,512,2048]{2,1,0:T(8,128)} fusion(bf16[1,16,512,2048]{3,2,1,0:T(8,128)(2,1)} %param.5), kind=kLoop, calls=%fused_computation | loop fusion | flops 16777216 | bytes 100663296 | tf_op jit(solution)/shard_map/convert_element_type | solution.py:45
  39.6 0.0 reduce-scatter.2.cloned.1.call-update
  39.7 626.6 %reduce-scatter.2.cloned.1.call-done = f32[16,32,2048]{2,1,0:T(8,128)} async-done(((f32[16,512,2048]{2,1,0:T(8,128)}), f32[16,32,2048]{2,1,0:T(8,128)}) %reduce-scatter.2.cloned.1.call-update) | async-done | bytes 4194320 | tf_op jit(solution)/shard_map/reduce_scatter | solution.py:45
  666.2 4.1 multiply_reduce_fusion
  670.4 0.0 copy-start
  670.4 2.0 copy-done
  672.4 1.6 convert_element_type.146
  674.0 6.7 all-to-all-start
  680.7 61.8 %psum.7 = f32[16]{0:T(128)S(1)} all-reduce(f32[16]{0:T(128)S(1)} %get-tuple-element.2), channel_id=1, replica_groups=mesh['stage'=2,'data'=16] {'data'}, use_global_device_ids=true, to_apply=%region_2.0 | all-reduce | flops 16 | bytes 128 | tf_op jit(solution)/shard_map/psum | solution.py:47
  742.5 0.7 dynamic_slice.3
  743.9 0.0 all-to-all-done
  743.9 0.4 divide_convert_fusion
  744.3 0.0 copy-start.2
  744.3 1.3 copy-done.2
  745.6 1.3 convolution_convert_fusion.4
  746.9 3.8 add_convert_fusion.4
  750.7 1.3 convolution_convert_fusion.3
  752.0 2.9 add_convert_fusion.3
  754.9 0.0 copy-start.3
  754.9 3.6 convolution_convert_fusion.2
  758.5 0.0 copy-done.3
  758.5 2.9 add_convert_fusion.2
  761.4 0.0 copy-start.4
  761.4 3.6 convolution_convert_fusion.1
  765.1 0.0 copy-done.4
  765.1 2.9 add_convert_fusion.1
  767.9 3.5 convolution_convert_fusion
  771.4 3.8 fusion
  775.2 5.4 copy.8
  780.6 0.6 broadcast.86
  781.2 13.2 %reduce = bf16[512,2048]{1,0:T(8,128)(2,1)S(1)} reduce(bf16[512,1,2048]{2,1,0:T(2,128)(2,1)} %bitcast.39, bf16[]{:T(256)} %broadcast.86), dimensions={1}, to_apply=%bitcast.37.reduce_sub_computation | reduce | bytes 4194306
  794.4 2.8 reshape.164
  797.2 55.5 %all_to_all.8 = bf16[16,2,32768]{2,1,0:T(2,128)(2,1)S(1)} all-to-all(bf16[16,2,32768]{2,1,0:T(2,128)(2,1)} %reshape.164), channel_id=1, replica_groups=mesh['stage'=2,'data'=16] {'data'}, dimensions={0} | all-to-all | bytes 4194304 | tf_op jit(solution)/shard_map/all_to_all | solution.py:52
  852.8 6.7 reshape.165
  859.5 7.9 convert_multiply_fusion
  867.4 0.0 copy-start.1
  867.4 2.0 copy.6
  869.4 0.2 copy-done.1
  869.6 3.0 multiply_subtract_fusion
  (1 shorter events, 0.0 us)
Async XLA Ops:
  7.2 659.1 %reduce-scatter.2.cloned.1.call-start = ((), (), s32[]{:S(2)}) async-start(), calls=%async_computation.3 | async-start | bytes 71303168 | tf_op jit(solution)/shard_map/reduce_scatter | solution.py:45
  670.4 2.0 copy-start
  674.0 69.9 %all-to-all-start = ((bf16[16,32,2048]{2,1,0:T(8,128)(2,1)}), bf16[16,32,2048]{2,1,0:T(8,128)(2,1)S(1)}, u32[]{:S(2)}, u32[]{:S(2)}) async-start(bf16[16,32,2048]{2,1,0:T(8,128)(2,1)} %convert_element_type.146), calls=%async_computation.1 | async-start | bytes 4194304 | tf_op jit(solution)/shard_map/all_to_all | solution.py:48
  744.3 1.3 copy-start.2
  754.9 3.7 copy-start.3
  761.4 3.7 copy-start.4
  867.4 2.2 copy-start.1
Sparse Core Ops, SparseCore 0:
  39.8 626.3 reduce-scatter.1
where the time goes:
time: 880 us; the launch traced here: 879 us
  waiting for transfers between devices  627 us (71%)
  blocking collectives  117 us (13%)
  other arithmetic  62.7 us (7%)
  matrix products  29.5 us (3%)
  local copies, waits for them, and re-layouts  21.7 us (2%)
  between operations  14.8 us (2%)
    reduce_scatter x1, waiting for transfers between devices, local_step(): lax.psum_scatter(grad_full[0].astype(jnp.float32), 'data', scatter_dimens...  627 us
    psum x1, blocking collectives, local_step(): lax.psum(jnp.sum(mom_new * mom_new, axis=(1, 2)), 'data')  61.8 us
    all_to_all x1, blocking collectives, local_step(): x_rows = lax.all_to_all(x_ortho, 'data', 1, 0, tiled=True)  55.5 us
    convert_element_type x1, other arithmetic, local_step(): grad_full[0].astype(jnp.float32)  32.4 us
  transfers between devices with their start and end apart: 2, of which 1 were waited for; matrix products, arithmetic and copies ran while one was open for 0% of the time, Pallas kernels for 0%

commit v1 on v0

v1 whole, which is shorter than its diff:
```python
import functools
import math
import jax
import jax.numpy as jnp
from jax import lax
from jax.experimental import pallas as pl
from jax.experimental.pallas import tpu as pltpu
from jax.sharding import PartitionSpec as P

MOMENTUM_COEF = 0.95
LEARN_RATE = 0.05
WEIGHT_DECAY = 0.2
NORM_EPS = 1e-7
COEF_A = 3.4445
COEF_B = -4.7750
COEF_C = 2.0315
NS_ITERS = 5

NZ, NY_, NC = 4, 2, 2
ROWS_B = 16
COLS_Z_FIRST = 256
LAG_Y = 1
LAG_R = 3
HOP = 2
LAG_X = 2
LAG_W = 4

N_P = 2 * LAG_Y + 2
N_S = 3
N_R = 2 * LAG_R + 3 * HOP + 3 - 2 * LAG_Y
N_H = 4 * HOP + 3
N_X = 4


def muon_kernel(n_mats, rows, cols, split, g_hbm, mom_hbm, w_hbm, mom_out, w_out,
                own, prt, ysend, tsum, yrecv, upr, dnr, tsb, upb, dnb, frv,
                momv, wv, xs, xv, ov, gram, poly, ssq_part, ssq_all,
                own_sem, p_ssem, p_rsem, y_ssem, y_rsem, u_ssem, u_rsem, d_ssem, d_rsem,
                ub_ssem, ub_rsem, db_ssem, db_rsem, f_ssem, f_rsem,
                x_ssem, x_rsem, q_ssem, q_rsem, o_ssem, o_rsem, l_sem, mo_sem, wo_sem):
    stage = lax.axis_index('stage')
    me = lax.axis_index('data')
    n_dev = NZ * NY_ * NC
    z = me // 4
    y = (me // 2) % 2
    c = me % 2
    per_mat = rows // ROWS_B
    chunks = n_mats * per_mat
    n_rows = rows * n_dev
    mine = ((3 * z) % 4) * 4 + me % 4
    rms_scale = 0.2 * math.sqrt(max(n_rows, cols))
    lag_z0 = LAG_R
    lag_f = LAG_R + 3 * HOP
    lag_bf = LAG_Y + 3 * HOP
    lag_w = lag_f + LAG_X + NS_ITERS + LAG_W

    def owner(m):
        return ((3 * (m // 4)) % 4) * 4 + m % 4

    def remote(src, dst, ssem, rsem, dev):
        return pltpu.make_async_remote_copy(
            src_ref=src, dst_ref=dst, send_sem=ssem, recv_sem=rsem,
            device_id=(stage, dev), device_id_type=pl.DeviceIdType.MESH)

    partner = z * 4 + y * 2 + (1 - c)
    ynbr = z * 4 + (1 - y) * 2 + c

    def g_slice(k, core):
        return g_hbm.at[k // per_mat, :, :, core, pl.ds((k % per_mat) * ROWS_B, ROWS_B), :]

    def own_copy(k):
        return pltpu.make_async_copy(g_slice(k, c), own.at[k % N_P], own_sem.at[k % N_P])

    def prt_copy(k):
        return remote(g_slice(k, 1 - c), prt.at[k % N_P], p_ssem.at[k % N_P], p_rsem.at[k % N_P], partner)

    def y_copy(k):
        return remote(ysend.at[k % N_S], yrecv.at[k % N_R], y_ssem.at[k % N_S], y_rsem.at[k % N_R], ynbr)

    def up_copy(k, zp):
        return remote(tsum.at[k % N_R, zp], upr.at[k % N_H, zp], u_ssem.at[k % N_R, zp], u_rsem.at[k % N_H, zp], me + 4)

    def dn_copy(k, zp):
        return remote(tsum.at[k % N_R, zp], dnr.at[k % N_H, zp], d_ssem.at[k % N_R, zp], d_rsem.at[k % N_H, zp], me - 4)

    def upb_copy(k, zp):
        return remote(tsb.at[k % N_R, zp], upb.at[k % N_H, zp], ub_ssem.at[k % N_R, zp], ub_rsem.at[k % N_H, zp], me + 4)

    def dnb_copy(k, zp):
        return remote(tsb.at[k % N_R, zp], dnb.at[k % N_H, zp], db_ssem.at[k % N_R, zp], db_rsem.at[k % N_H, zp], me - 4)

    def f_copy(k):
        return remote(tsb.at[k % N_R, z, 1 - y], frv.at[k % N_R], f_ssem.at[k % N_R], f_rsem.at[k % N_R], ynbr)

    def x_copy(k):
        m = k // per_mat
        r0 = (k % per_mat) * ROWS_B
        return remote(xs.at[k % N_X], xv.at[pl.ds(me * rows + r0, ROWS_B), :], x_ssem.at[k % N_X], x_rsem, owner(m))

    def q_copy(m):
        return remote(ssq_part.at[m], ssq_all.at[me], q_ssem, q_rsem, owner(m))

    def o_copy(dev):
        return remote(xv.at[pl.ds(dev * rows, rows), :], ov.at[mine], o_ssem, o_rsem.at[mine], dev)

    def mo_copy(k):
        m = k // per_mat
        rs = pl.ds((k % per_mat) * ROWS_B, ROWS_B)
        return pltpu.make_async_copy(momv.at[m, rs, :], mom_out.at[m, rs, :], mo_sem)

    mom_in = pltpu.make_async_copy(mom_hbm, momv, l_sem.at[0])
    w_in = pltpu.make_async_copy(w_hbm, wv, l_sem.at[1])

    barrier = pltpu.get_barrier_semaphore()

    def greet(i, carry):
        pl.semaphore_signal(barrier, inc=1, device_id=(stage, (me + i) % n_dev), device_id_type=pl.DeviceIdType.MESH)
        return carry

    lax.fori_loop(1, n_dev, greet, 0)

    @pl.when(z == 0)
    def _():
        upr[...] = jnp.zeros_like(upr)
        upb[...] = jnp.zeros_like(upb)

    @pl.when(z == NZ - 1)
    def _():
        dnr[...] = jnp.zeros_like(dnr)
        dnb[...] = jnp.zeros_like(dnb)

    pl.semaphore_wait(barrier, n_dev - 1)

    def at(k, lo=0, hi=chunks):
        return jnp.logical_and(k >= lo, k < hi)

    def step(s, carry):
        @pl.when(s < chunks)
        def _():
            own_copy(s).start()
            prt_copy(s).start()

        @pl.when(s == 1)
        def _():
            mom_in.start()

        @pl.when(s == 4)
        def _():
            w_in.start()

        ky = s - LAG_Y

        @pl.when(at(ky, N_S, chunks + N_S))
        def _():
            y_copy(ky - N_S).wait_send()

        @pl.when(at(ky, N_R, chunks + N_R))
        def _():
            for zp in range(NZ):
                @pl.when(zp > z)
                def _():
                    up_copy(ky - N_R, zp).wait_send()
                    upb_copy(ky - N_R, zp).wait_send()

                @pl.when(zp < z)
                def _():
                    dn_copy(ky - N_R, zp).wait_send()
                    dnb_copy(ky - N_R, zp).wait_send()
            f_copy(ky - N_R).wait_send()

        @pl.when(at(ky))
        def _():
            own_copy(ky).wait()
            prt_copy(ky).wait_send()
            prt_copy(ky).wait_recv()
            ip, it = ky % N_P, ky % N_R

            def other(zp, carry):
                ysend[ky % N_S, zp] = (own[ip, zp, 1 - y, :, :split].astype(jnp.float32)
                                       + prt[ip, zp, 1 - y, :, :split].astype(jnp.float32))
                return carry

            def same(zp, carry):
                tsum[it, zp] = (own[ip, zp, y, :, :split].astype(jnp.float32)
                                + prt[ip, zp, y, :, :split].astype(jnp.float32))
                for yp in range(NY_):
                    tsb[it, zp, yp] = (own[ip, zp, yp, :, split:].astype(jnp.float32)
                                       + prt[ip, zp, yp, :, split:].astype(jnp.float32))
                return carry

            lax.fori_loop(0, NZ, other, 0)
            lax.fori_loop(0, NZ, same, 0)
            y_copy(ky).start()

        kbu = s - LAG_Y - HOP * z

        @pl.when(at(kbu))
        def _():
            for zp in range(1, NZ):
                @pl.when(zp > z)
                def _():
                    @pl.when(z > 0)
                    def _():
                        upb_copy(kbu, zp).wait_recv()
                    tsb[kbu % N_R, zp] += upb[kbu % N_H, zp]
            for zp in range(NZ - 1, 0, -1):
                @pl.when(zp > z)
                def _():
                    upb_copy(kbu, zp).start()

        kbd = s - LAG_Y - HOP * (NZ - 1 - z)

        @pl.when(at(kbd))
        def _():
            for zp in range(NZ - 1):
                @pl.when(zp < z)
                def _():
                    @pl.when(z < NZ - 1)
                    def _():
                        dnb_copy(kbd, zp).wait_recv()
                    tsb[kbd % N_R, zp] += dnb[kbd % N_H, zp]
            for zp in range(NZ - 1):
                @pl.when(zp < z)
                def _():
                    dnb_copy(kbd, zp).start()

        kbf = s - lag_bf

        @pl.when(at(kbf))
        def _():
            @pl.when(z > 0)
            def _():
                upb_copy(kbf, z).wait_recv()

            @pl.when(z < NZ - 1)
            def _():
                dnb_copy(kbf, z).wait_recv()
            tsb[kbf % N_R, z] += upb[kbf % N_H, z] + dnb[kbf % N_H, z]
            f_copy(kbf).start()

        kr = s - LAG_R

        @pl.when(at(kr))
        def _():
            y_copy(kr).wait_recv()

        ku = s - lag_z0 - HOP * z

        @pl.when(at(ku))
        def _():
            for zp in range(NZ - 1, 0, -1):
                @pl.when(zp > z)
                def _():
                    @pl.when(z > 0)
                    def _():
                        up_copy(ku, zp).wait_recv()
                    tsum[ku % N_R, zp] += yrecv[ku % N_R, zp] + upr[ku % N_H, zp]
            for zp in range(NZ - 1, 0, -1):
                @pl.when(zp > z)
                def _():
                    up_copy(ku, zp).start()

        kd = s - lag_z0 - HOP * (NZ - 1 - z)

        @pl.when(at(kd))
        def _():
            for zp in range(NZ - 1):
                @pl.when(zp < z)
                def _():
                    @pl.when(z < NZ - 1)
                    def _():
                        dn_copy(kd, zp).wait_recv()
                    tsum[kd % N_R, zp] += yrecv[kd % N_R, zp] + dnr[kd % N_H, zp]
            for zp in range(NZ - 1):
                @pl.when(zp < z)
                def _():
                    dn_copy(kd, zp).start()

        kf = s - lag_f

        @pl.when(kf == 0)
        def _():
            mom_in.wait()
            ssq_part[...] = jnp.zeros_like(ssq_part)

        @pl.when(at(kf, N_X, chunks + N_X))
        def _():
            kx = kf - N_X

            @pl.when(owner(kx // per_mat) != me)
            def _():
                x_copy(kx).wait_send()

        @pl.when(at(kf))
        def _():
            @pl.when(z > 0)
            def _():
                up_copy(kf, z).wait_recv()

            @pl.when(z < NZ - 1)
            def _():
                dn_copy(kf, z).wait_recv()
            f_copy(kf).wait_recv()
            m = kf // per_mat
            r0 = pl.multiple_of((kf % per_mat) * ROWS_B, ROWS_B)
            it, ih = kf % N_R, kf % N_H
            g_a = (tsum[it, z] + yrecv[it, z]) + (upr[ih, z] + dnr[ih, z])
            m_a = MOMENTUM_COEF * momv[m, pl.ds(r0, ROWS_B), :split] + g_a
            momv[m, pl.ds(r0, ROWS_B), :split] = m_a
            xs[kf % N_X, :, :split] = m_a.astype(jnp.bfloat16)
            g_b = tsb[it, z, y] + frv[it]
            m_b = MOMENTUM_COEF * momv[m, pl.ds(r0, ROWS_B), split:] + g_b
            momv[m, pl.ds(r0, ROWS_B), split:] = m_b
            xs[kf % N_X, :, split:] = m_b.astype(jnp.bfloat16)
            sq_a, sq_b = m_a * m_a, m_b * m_b
            part = ssq_part[m]
            for r in range(0, ROWS_B, 8):
                for j in range(0, split, 128):
                    part = part + sq_a[r:r + 8, j:j + 128]
                for j in range(0, cols - split, 128):
                    part = part + sq_b[r:r + 8, j:j + 128]
            ssq_part[m] = part
            mo_copy(kf).start()
            last = kf % per_mat == per_mat - 1

            @pl.when(owner(m) == me)
            def _():
                xv[pl.ds(pl.multiple_of(me * rows + r0, ROWS_B), ROWS_B), :] = xs[kf % N_X]

                @pl.when(last)
                def _():
                    ssq_all[me] = ssq_part[m]

            @pl.when(owner(m) != me)
            def _():
                x_copy(kf).start()

                @pl.when(last)
                def _():
                    q_copy(m).start()

        q = s - ((mine + 1) * per_mat - 1 + lag_f + LAG_X)

        @pl.when(q == 0)
        def _():
            others = pl.ds(0, (n_dev - 1) * rows)
            pltpu.make_async_copy(xv.at[others, :], xv.at[others, :], x_rsem).wait()
            parts = pl.ds(0, n_dev - 1)
            pltpu.make_async_copy(ssq_all.at[parts], ssq_all.at[parts], q_rsem).wait()
            nrm = jnp.sqrt(jnp.sum(jnp.sum(ssq_all[...], axis=0), keepdims=True))
            inv = 1.0 / (nrm + NORM_EPS)

            def scale(i, carry):
                rs = pl.ds(pl.multiple_of(i * 32, 32), 32)
                xv[rs, :] = (xv[rs, :].astype(jnp.float32) * inv).astype(jnp.bfloat16)
                return carry

            lax.fori_loop(0, n_rows // 32, scale, 0)

        @pl.when(at(q, 1, NS_ITERS + 1))
        def _():
            tile = 256

            def gram_tile(j, carry):
                js = pl.ds(pl.multiple_of(j * tile, tile), tile)
                gram[:, js] = lax.dot_general(
                    xv[...], xv[js, :], (((1,), (1,)), ((), ())),
                    preferred_element_type=jnp.float32).astype(jnp.bfloat16)
                return carry

            def poly_tile(j, carry):
                js = pl.ds(pl.multiple_of(j * tile, tile), tile)
                sq = jnp.dot(gram[...], gram[:, js], preferred_element_type=jnp.float32)
                poly[:, js] = (COEF_B * gram[:, js].astype(jnp.float32) + COEF_C * sq).astype(jnp.bfloat16)
                return carry

            def x_tile(j, carry):
                js = pl.ds(pl.multiple_of(j * tile, tile), tile)
                px = jnp.dot(poly[...], xv[:, js], preferred_element_type=jnp.float32)
                xv[:, js] = (COEF_A * xv[:, js].astype(jnp.float32) + px).astype(jnp.bfloat16)
                return carry

            lax.fori_loop(0, n_rows // tile, gram_tile, 0)
            lax.fori_loop(0, n_rows // tile, poly_tile, 0)
            lax.fori_loop(0, cols // tile, x_tile, 0)

        @pl.when(q == NS_ITERS)
        def _():
            def give(i, carry):
                o_copy((me + i) % n_dev).start()
                return carry

            lax.fori_loop(1, n_dev, give, 0)
            ov[mine] = xv[pl.ds(pl.multiple_of(me * rows, rows), rows), :]

        kw = s - lag_w

        @pl.when(kw == 0)
        def _():
            w_in.wait()

        @pl.when(jnp.logical_and(at(kw), kw % per_mat == per_mat - 1))
        def _():
            m = kw // per_mat

            @pl.when(owner(m) != me)
            def _():
                remote(ov.at[m], ov.at[m], o_ssem, o_rsem.at[m], me).wait_recv()

            w = wv[m]
            wv[m] = w - LEARN_RATE * (ov[m].astype(jnp.float32) * rms_scale + WEIGHT_DECAY * w)
            pltpu.make_async_copy(wv.at[m], w_out.at[m], wo_sem).start()

        return carry

    lax.fori_loop(0, chunks + lag_w, step, 0)
    pltpu.make_async_copy(momv, mom_out, mo_sem).wait()
    pltpu.make_async_copy(wv, w_out, wo_sem).wait()
    others = pl.ds(0, (n_dev - 1) * rows)
    pltpu.make_async_copy(xv.at[others, :], xv.at[others, :], o_ssem).wait()
    sent = pl.ds(0, n_mats - 1)
    pltpu.make_async_copy(ssq_part.at[sent], ssq_part.at[sent], q_ssem).wait()


def solution(mesh):
    row_spec = P('stage', 'data', None)
    grad_spec = P(('stage', 'data'), None, None, None)
    f32, bf16 = jnp.float32, jnp.bfloat16

    def local_step(w_rows, mom_rows, grad_full):
        n_mats, rows, cols = w_rows.shape
        n_rows = grad_full.shape[2]
        split = cols - COLS_Z_FIRST
        g = grad_full.reshape(n_mats, NZ, NY_, NC, rows, cols)
        rb, cb = ROWS_B, COLS_Z_FIRST
        dma = pltpu.SemaphoreType.DMA
        scratch = [
            pltpu.VMEM((N_P, NZ, NY_, rb, cols), bf16),
            pltpu.VMEM((N_P, NZ, NY_, rb, cols), bf16),
            pltpu.VMEM((N_S, NZ, rb, split), f32),
            pltpu.VMEM((N_R, NZ, rb, split), f32),
            pltpu.VMEM((N_R, NZ, rb, split), f32),
            pltpu.VMEM((N_H, NZ, rb, split), f32),
            pltpu.VMEM((N_H, NZ, rb, split), f32),
            pltpu.VMEM((N_R, NZ, NY_, rb, cb), f32),
            pltpu.VMEM((N_H, NZ, NY_, rb, cb), f32),
            pltpu.VMEM((N_H, NZ, NY_, rb, cb), f32),
            pltpu.VMEM((N_R, rb, cb), f32),
            pltpu.VMEM((n_mats, rows, cols), f32),
            pltpu.VMEM((n_mats, rows, cols), f32),
            pltpu.VMEM((N_X, rb, cols), bf16),
            pltpu.VMEM((n_rows, cols), bf16),
            pltpu.VMEM((n_mats, rows, cols), bf16),
            pltpu.VMEM((n_rows, n_rows), bf16),
            pltpu.VMEM((n_rows, n_rows), bf16),
            pltpu.VMEM((n_mats, 8, 128), f32),
            pltpu.VMEM((NZ * NY_ * NC, 8, 128), f32),
            dma((N_P,)), dma((N_P,)), dma((N_P,)), dma((N_S,)), dma((N_R,)),
            dma((N_R, NZ)), dma((N_H, NZ)), dma((N_R, NZ)), dma((N_H, NZ)),
            dma((N_R, NZ)), dma((N_H, NZ)), dma((N_R, NZ)), dma((N_H, NZ)),
            dma((N_R,)), dma((N_R,)),
            dma((N_X,)), dma(()), dma(()), dma(()), dma(()), dma((n_mats,)),
            dma((2,)), dma(()), dma(()),
        ]
        hbm = pl.BlockSpec(memory_space=pltpu.HBM)
        mom_new, w_new = pl.pallas_call(
            functools.partial(muon_kernel, n_mats, rows, cols, split),
            out_shape=[jax.ShapeDtypeStruct(w_rows.shape, f32)] * 2,
            in_specs=[hbm] * 3,
            out_specs=[hbm] * 2,
            scratch_shapes=scratch,
            compiler_params=pltpu.CompilerParams(
                collective_id=0, has_side_effects=True, vmem_limit_bytes=60 * 1024 * 1024),
            name='muon',
        )(g, mom_rows, w_rows)
        return w_new, mom_new

    return jax.shard_map(local_step, mesh=mesh, in_specs=(row_spec, row_spec, grad_spec), out_specs=(row_spec, row_spec), check_vma=False)
```

time: 880 us -> 528 us (0.60)
  the two profiles are of different devices: /device:TPU:9 before, /device:TPU:31 now
where the time goes in v1:
time: 528 us
  Pallas kernels  520 us (98%)
  local copies, waits for them, and re-layouts  6.87 us (1%)
    pallas_call x1, Pallas kernels, local_step(): pl.pallas_call(functools.partial(muon_kernel, n_mats, rows, cols, split),...  520 us

profile of v1, /device:TPU:31, one launch (start us, length us, event | category | flops | bytes accessed | tf_op | source)
XLA Modules:
  0.0 527.9 jit_solution(11778441340178474961)
XLA Ops:
  0.6 520.4 %muon.1 = (f32[16,32,2048]{2,1,0:T(8,128)}, f32[16,32,2048]{2,1,0:T(8,128)}) custom-call(bf16[16,4,2,2,32,2048]{5,4,3,2,1,0:T(8,128)(2,1)} %bitcast.1, f32[16,32,2048]{2,1,0:T(8,128)} %mom_hbm.1, f32[16,32,2048]{2,1,0:T(8,128)} %w_hbm.1), custom_call_target="tpu_custom_call" | custom-call | tf_op jit(solution)/shard_map/muon/pallas_call | solution.py:466
  521.0 0.0 copy-start
  521.0 4.8 copy.7
  525.9 0.0 copy-done
  525.9 2.0 copy.8
Async XLA Ops:
  521.0 4.9 copy-start
